TPU v7x, 32 devices: a whole 2x2x4 slice. The times are simulated.
32 devices in a mesh: grp: 2 (over y), gx: 16 (over z, x, core), gy: 1.
Axes of the slice: x: 2, y: 2, z: 4, core: 2. Of those that a mesh axis runs over, the one named last changes fastest.
Arguments:
- residue_feats: bfloat16 [512, 256], P(('grp', 'gx')), parts along dimension 0, may hold values from -6 to 6
- pair_feats: bfloat16 [64, 512, 256], P(None, ('grp', 'gx'), 'gy'), parts along dimension 1, may hold values from -30 to 30
- w_row: bfloat16 [256, 64], replicated, may hold values from -0.375 to 0.375
- w_col: bfloat16 [256, 64], replicated, may hold values from -0.375 to 0.375
- first_taps: bfloat16 [9, 64, 64], replicated, may hold values from -0.25 to 0.25
- second_taps: bfloat16 [9, 64, 64], replicated, may hold values from -0.25 to 0.25
- norm_scale: float32 [2, 64], replicated, may hold values from 0.25 to 1.75
- norm_shift: float32 [2, 64], replicated, may hold values from -2 to 2
Outputs:
- symmetric: bfloat16 [64, 512, 256], P(None, ('grp', 'gx'), 'gy'), parts along dimension 1
There are 2 independent parts, one for each index of `grp`. A program takes and returns all parts, laid end to end along the dimension named above; an argument that names none is the same for every part. Nothing has to cross between parts.
All inputs are finite; a program needn't handle non-finite values.
Results may differ from a plain program's by a relative error of at most 0.012.
Values may be sent and summed in bfloat16 or wider, within the bound.
A program may use at most 64 MiB of HBM per device.

v0:
```python
import jax
import jax.numpy as jnp
from jax import lax
from jax.sharding import PartitionSpec as P

DILATION_STEP = 8
epsilon = 1e-05


def with_halo(cells, sides, width):
    for axis, dim in sides:
        count = lax.axis_size(axis)
        ends = count - 1
        head = lax.slice_in_dim(cells, 0, width, axis=dim)
        tail = lax.slice_in_dim(cells, cells.shape[dim] - width, cells.shape[dim], axis=dim)
        cells = jnp.concatenate(
            [
                lax.ppermute(tail, axis, [(i, (i + 1) % count) for i in range(ends)]),
                cells,
                lax.ppermute(head, axis, [((i + 1) % count, i) for i in range(ends)]),
            ],
            axis=dim,
        )
    return cells


def dilated(receptive_region, weights):
    row_count = receptive_region.shape[1]
    col_count = receptive_region.shape[2]
    border_padded_input = with_halo(receptive_region, (("gx", 1), ("gy", 2)), DILATION_STEP)
    tap_sum_total = jnp.zeros((weights.shape[1], row_count, col_count), jnp.float32)
    for filter_tap_index in range(9):
        row_displacement = filter_tap_index // 3 * DILATION_STEP
        column_displacement = filter_tap_index % 3 * DILATION_STEP
        window = border_padded_input[
            :,
            row_displacement : row_displacement + row_count,
            column_displacement : column_displacement + col_count,
        ]
        tap_sum_total = tap_sum_total + jnp.einsum(
            "oc,crw->orw", weights[filter_tap_index], window, preferred_element_type=jnp.float32
        )
    return tap_sum_total


def normalized(tap_sum_total, gain, shift):
    cell_count = (
        tap_sum_total.shape[1] * tap_sum_total.shape[2] * lax.axis_size("gx") * lax.axis_size("gy")
    )
    first_sum, second_sum = lax.psum(
        (jnp.sum(tap_sum_total, axis=(1, 2)), jnp.sum(tap_sum_total * tap_sum_total, axis=(1, 2))),
        ("gx", "gy"),
    )
    average = first_sum / cell_count
    spread = second_sum / cell_count - average * average
    centred = tap_sum_total - average[:, None, None]
    factor = gain * lax.rsqrt(spread + epsilon)
    return centred * factor[:, None, None] + shift[:, None, None]


def body(residue_feats, pair_feats, w_row, w_col, first_taps, second_taps, norm_scale, norm_shift):
    col_count = pair_feats.shape[2]
    col_start = lax.axis_index("gy") * col_count
    row_part = jnp.dot(residue_feats, w_row, preferred_element_type=jnp.float32).astype(
        jnp.bfloat16
    )
    everyone = lax.all_gather(residue_feats, "gx", axis=0, tiled=True)
    col_feats = lax.dynamic_slice_in_dim(everyone, col_start, col_count, 0)
    col_part = jnp.dot(col_feats, w_col, preferred_element_type=jnp.float32).astype(jnp.bfloat16)
    block_in = (
        pair_feats.astype(jnp.float32)
        + row_part.T.astype(jnp.float32)[:, :, None]
        + col_part.T.astype(jnp.float32)[:, None, :]
    ).astype(jnp.bfloat16)
    first_conv = dilated(block_in, first_taps)
    activated = jax.nn.elu(normalized(first_conv, norm_scale[0], norm_shift[0])).astype(
        jnp.bfloat16
    )
    second_conv = dilated(activated, second_taps)
    block_out = jax.nn.elu(
        block_in.astype(jnp.float32) + normalized(second_conv, norm_scale[1], norm_shift[1])
    ).astype(jnp.bfloat16)
    whole_rows = lax.all_gather(block_out, "gy", axis=2, tiled=True)
    columns = lax.all_to_all(whole_rows, "gx", split_axis=2, concat_axis=1, tiled=True)
    flipped = lax.dynamic_slice_in_dim(columns, col_start, col_count, 1)
    mirrored = jnp.transpose(flipped, (0, 2, 1))
    return (0.5 * (block_out.astype(jnp.float32) + mirrored.astype(jnp.float32))).astype(
        jnp.bfloat16
    )


def solution(mesh):
    placed = (P(("grp", "gx"), None), P(None, ("grp", "gx"), "gy"), P(), P(), P(), P(), P(), P())
    return jax.shard_map(
        body, mesh=mesh, in_specs=placed, out_specs=P(None, ("grp", "gx"), "gy"), check_vma=False
    )
```

profile of v0, /device:TPU:0, one launch (start us, length us, event | category | flops | bytes accessed | tf_op | source)
XLA Modules:
  0.0 140.1 jit_solution(18333366935052121485)
XLA Ops:
  0.0 0.0 copy-start
  0.0 23.8 %all_gather.4 = bf16[256,256]{1,0:T(8,128)(2,1)S(1)} all-gather(bf16[16,256]{1,0:T(8,128)(2,1)} %param.8), channel_id=1, replica_groups=mesh['grp'=2,'gx'=16,'gy'=1] {'gx'}, dimensions={0}, use_global_device_ids=true | all-gather | bytes 139264 | tf_op jit(solution)/shard_map/all_gather | solution.py:67
  23.8 0.9 fusion.13
  24.7 0.2 fusion.12
  24.9 1.3 add_convert_fusion
  26.2 2.3 %collective-permute-start = (bf16[64,8,256]{2,0,1:T(8,128)(2,1)S(1)}, bf16[64,8,256]{2,0,1:T(8,128)(2,1)S(1)}, u32[]{:S(2)}, u32[]{:S(2)}) collective-permute-start(bf16[64,8,256]{2,0,1:T(8,128)(2,1)S(1)} %get-tuple-element.23), channel_id=1, source_target_pairs={{0,1},{1,2},{2,3},{3,4},{4,5},{5,6},{6,7},{7,8},{8,9},{9,10},{10,1... | collective-permute-start | bytes 786440 | tf_op jit(solution)/shard_map/ppermute | solution.py:18
  28.5 1.3 collective-permute-start.1
  29.8 0.0 copy-done.5
  29.8 0.3 fusion.62
  30.1 0.0 collective-permute-done
  30.1 1.8 %collective-permute-done.1 = bf16[64,8,256]{2,0,1:T(8,128)(2,1)S(1)} collective-permute-done((bf16[64,8,256]{2,0,1:T(8,128)(2,1)S(1)}, bf16[64,8,256]{2,0,1:T(8,128)(2,1)S(1)}, u32[]{:S(2)}, u32[]{:S(2)}) %collective-permute-start.1) | collective-permute-done | bytes 262176 | tf_op jit(solution)/shard_map/ppermute | solution.py:20
  31.9 0.1 pad_maximum_fusion.2
  32.1 0.3 fusion.93
  32.3 0.7 collective-permute-start.2
  33.0 0.7 collective-permute-start.3
  33.7 0.3 fusion.45
  34.0 0.3 fusion.36
  34.3 0.0 collective-permute-done.2
  34.3 0.0 collective-permute-done.3
  34.3 1.3 maximum_maximum_fusion
  35.6 0.4 fusion.43
  36.0 0.4 fusion.34
  36.4 0.3 fusion.41
  36.7 0.3 fusion.38
  36.9 0.4 fusion.11
  37.3 0.0 copy-start.4
  37.3 0.7 fusion.91
  38.0 0.0 copy-start.3
  38.0 33.9 %all-reduce.1 = (f32[64]{0:T(128)S(1)}, f32[64]{0:T(128)S(1)}) all-reduce(f32[64]{0:T(128)S(1)} %get-tuple-element.8, f32[64]{0:T(128)S(1)} %get-tuple-element.7), channel_id=1, replica_groups=mesh['grp'=2,'gx'=16,'gy'=1] {'gx','gy'}, use_global_device_ids=true, to_apply=%region_3.0 | all-reduce | flops 128 | bytes 1024 | tf_op jit(solution)/shard_map/psum | solution.py:50
  72.0 0.0 copy-done.4
  72.0 0.6 fusion.15
  72.6 1.3 collective-permute-start.4
  73.9 1.3 collective-permute-start.5
  75.2 0.3 fusion.52
  75.5 0.0 collective-permute-done.4
  75.5 1.8 %collective-permute-done.5 = bf16[64,8,256]{2,0,1:T(8,128)(2,1)S(1)} collective-permute-done((bf16[64,8,256]{2,0,1:T(8,128)(2,1)S(1)}, bf16[64,8,256]{2,0,1:T(8,128)(2,1)S(1)}, u32[]{:S(2)}, u32[]{:S(2)}) %collective-permute-start.5) | collective-permute-done | bytes 262176 | tf_op jit(solution)/shard_map/ppermute | solution.py:20
  77.4 0.1 pad_maximum_fusion.3
  77.5 0.3 fusion.92
  77.8 0.7 collective-permute-start.6
  78.5 0.7 collective-permute-start.7
  79.2 0.3 fusion.31
  79.4 0.3 fusion.22
  79.7 0.0 collective-permute-done.6
  79.7 0.0 collective-permute-done.7
  79.7 1.3 maximum_maximum_fusion.1
  81.0 0.4 fusion.29
  81.4 0.4 fusion.20
  81.8 0.3 fusion.27
  82.1 0.3 fusion.24
  82.3 0.4 fusion.5
  82.7 0.0 copy-start.1
  82.8 0.7 fusion.90
  83.4 31.5 %all-reduce = (f32[64]{0:T(128)S(1)}, f32[64]{0:T(128)S(1)}) all-reduce(f32[64]{0:T(128)S(1)} %get-tuple-element.6, f32[64]{0:T(128)S(1)} %get-tuple-element.5), channel_id=1, replica_groups=mesh['grp'=2,'gx'=16,'gy'=1] {'gx','gy'}, use_global_device_ids=true, to_apply=%region_7.8 | all-reduce | flops 128 | bytes 1024 | tf_op jit(solution)/shard_map/psum | solution.py:50
  115.0 0.7 fusion.17
  115.7 1.0 copy.18
  116.7 0.7 reshape.32
  117.4 16.9 %all_to_all.4 = bf16[16,2,8192]{2,1,0:T(2,128)(2,1)S(1)} all-to-all(bf16[16,2,8192]{2,1,0:T(2,128)(2,1)S(1)} %reshape.32), channel_id=1, replica_groups=mesh['grp'=2,'gx'=16,'gy'=1] {'gx'}, dimensions={0} | all-to-all | bytes 1048576 | tf_op jit(solution)/shard_map/all_to_all | solution.py:84
  134.3 0.7 reshape.33
  135.0 0.3 copy.19
  135.2 0.2 convert_bitcast_fusion
  135.5 0.2 copy.20
  135.7 2.0 %copy.21 = f32[64,256,16]{1,0,2:T(8,128)} copy(f32[64,256,16]{0,2,1:T(8,128)S(1)} %bitcast.109) | data formatting | bytes 2097152 | tf_op jit(solution)/shard_map/convert_element_type | solution.py:87
  137.6 1.4 fusion.19
  139.0 1.1 copy.22
  (11 shorter events, 0.1 us)
Async XLA Ops:
  0.0 24.7 %copy-start = (bf16[256,64]{0,1:T(8,128)(2,1)S(1)}, bf16[256,64]{0,1:T(8,128)(2,1)}, u32[]{:S(2)}) copy-start(bf16[256,64]{0,1:T(8,128)(2,1)} %param.11) | copy-start | bytes 98308
  0.0 29.8 %copy-start.5 = (f32[2,64]{1,0:T(2,128)S(1)}, f32[2,64]{1,0:T(2,128)}, u32[]{:S(2)}) copy-start(f32[2,64]{1,0:T(2,128)} %param.15) | copy-start | bytes 1540
  0.0 29.8 %copy-start.2 = (bf16[9,64,64]{2,1,0:T(8,128)(2,1)S(1)}, bf16[9,64,64]{2,1,0:T(8,128)(2,1)}, u32[]{:S(2)}) copy-start(bf16[9,64,64]{2,1,0:T(8,128)(2,1)} %param.12) | copy-start | bytes 221188
  26.2 3.9 %collective-permute-start = (bf16[64,8,256]{2,0,1:T(8,128)(2,1)S(1)}, bf16[64,8,256]{2,0,1:T(8,128)(2,1)S(1)}, u32[]{:S(2)}, u32[]{:S(2)}) collective-permute-start(bf16[64,8,256]{2,0,1:T(8,128)(2,1)S(1)} %get-tuple-element.23), channel_id=1, source_target_pairs={{0,1},{1,2},{2,3},{3,4},{4,5},{5,6},{6,7},{7,8},{8,9},{9,10},{10,1... | collective-permute-start | bytes 786440 | tf_op jit(solution)/shard_map/ppermute | solution.py:18
  28.5 3.4 %collective-permute-start.1 = (bf16[64,8,256]{2,0,1:T(8,128)(2,1)S(1)}, bf16[64,8,256]{2,0,1:T(8,128)(2,1)S(1)}, u32[]{:S(2)}, u32[]{:S(2)}) collective-permute-start(bf16[64,8,256]{2,0,1:T(8,128)(2,1)S(1)} %get-tuple-element.24), channel_id=1, source_target_pairs={{1,0},{2,1},{3,2},{4,3},{5,4},{6,5},{7,6},{8,7},{9,8},{10,9},{11,1... | collective-permute-start | bytes 786440 | tf_op jit(solution)/shard_map/ppermute | solution.py:20
  32.3 1.9 %collective-permute-start.2 = (bf16[64,32,8]{2,0,1:T(8,128)(2,1)S(1)}, bf16[64,32,8]{2,0,1:T(8,128)(2,1)S(1)}, u32[]{:S(2)}, u32[]{:S(2)}) collective-permute-start(bf16[64,32,8]{2,0,1:T(8,128)(2,1)S(1)} %get-tuple-element.19), channel_id=1, source_target_pairs={} | collective-permute-start | bytes 98312 | tf_op jit(solution)/shard_map/ppermute | solution.py:18
  33.0 1.3 collective-permute-start.3
  37.3 34.6 %copy-start.4 = (f32[2,64]{1,0:T(2,128)S(1)}, f32[2,64]{1,0:T(2,128)}, u32[]{:S(2)}) copy-start(f32[2,64]{1,0:T(2,128)} %param.14) | copy-start | bytes 1540
  38.0 37.2 %copy-start.3 = (bf16[9,64,64]{2,1,0:T(8,128)(2,1)S(1)}, bf16[9,64,64]{2,1,0:T(8,128)(2,1)}, u32[]{:S(2)}) copy-start(bf16[9,64,64]{2,1,0:T(8,128)(2,1)} %param.13) | copy-start | bytes 221188
  72.6 2.9 %collective-permute-start.4 = (bf16[64,8,256]{2,0,1:T(8,128)(2,1)S(1)}, bf16[64,8,256]{2,0,1:T(8,128)(2,1)S(1)}, u32[]{:S(2)}, u32[]{:S(2)}) collective-permute-start(bf16[64,8,256]{2,0,1:T(8,128)(2,1)S(1)} %get-tuple-element.21), channel_id=1, source_target_pairs={{0,1},{1,2},{2,3},{3,4},{4,5},{5,6},{6,7},{7,8},{8,9},{9,10},{10,1... | collective-permute-start | bytes 786440 | tf_op jit(solution)/shard_map/ppermute | solution.py:18
  73.9 3.4 %collective-permute-start.5 = (bf16[64,8,256]{2,0,1:T(8,128)(2,1)S(1)}, bf16[64,8,256]{2,0,1:T(8,128)(2,1)S(1)}, u32[]{:S(2)}, u32[]{:S(2)}) collective-permute-start(bf16[64,8,256]{2,0,1:T(8,128)(2,1)S(1)} %get-tuple-element.22), channel_id=1, source_target_pairs={{1,0},{2,1},{3,2},{4,3},{5,4},{6,5},{7,6},{8,7},{9,8},{10,9},{11,1... | collective-permute-start | bytes 786440 | tf_op jit(solution)/shard_map/ppermute | solution.py:20
  77.8 1.9 %collective-permute-start.6 = (bf16[64,32,8]{2,0,1:T(8,128)(2,1)S(1)}, bf16[64,32,8]{2,0,1:T(8,128)(2,1)S(1)}, u32[]{:S(2)}, u32[]{:S(2)}) collective-permute-start(bf16[64,32,8]{2,0,1:T(8,128)(2,1)S(1)} %get-tuple-element.15), channel_id=1, source_target_pairs={} | collective-permute-start | bytes 98312 | tf_op jit(solution)/shard_map/ppermute | solution.py:18
  78.5 1.3 collective-permute-start.7
  82.7 32.2 %copy-start.1 = (bf16[64,16,256]{2,1,0:T(8,128)(2,1)S(1)}, bf16[64,16,256]{2,1,0:T(8,128)(2,1)}, u32[]{:S(2)}) copy-start(bf16[64,16,256]{2,1,0:T(8,128)(2,1)} %param.9) | copy-start | bytes 1572868
where the time goes:
time: 141 us; the launch traced here: 140 us
  blocking collectives  106 us (75%)
  starting transfers between devices  8.9 us (6%)
  matrix products  7.38 us (5%)
  other arithmetic  7.08 us (5%)
  local copies, waits for them, and re-layouts  6.52 us (5%)
  waiting for transfers between devices  3.66 us (3%)
    psum x2, blocking collectives, normalized(): lax.psum((jnp.sum(tap_sum_total, axis=(1, 2)), jnp.sum(tap_sum_total * ta...  65.5 us
    all_gather x1, blocking collectives, body(): everyone = lax.all_gather(residue_feats, 'gx', axis=0, tiled=True)  23.8 us
    all_to_all x1, blocking collectives, body(): lax.all_to_all(whole_rows, 'gx', split_axis=2, concat_axis=1, tiled=True)  16.9 us
    dot_general x18, matrix products, dilated(): jnp.einsum('oc,crw->orw', weights[filter_tap_index], window, preferred_el...  6.34 us
    ppermute x4, starting transfers between devices, with_halo(): lax.ppermute(tail, axis, [(i, (i + 1) % count) for i in range(ends)])  4.94 us
    ppermute x4, starting transfers between devices, with_halo(): lax.ppermute(head, axis, [((i + 1) % count, i) for i in range(ends)])  3.96 us
    ppermute x4, waiting for transfers between devices, with_halo(): lax.ppermute(head, axis, [((i + 1) % count, i) for i in range(ends)])  3.65 us
    concatenate x4, other arithmetic, with_halo(): jnp.concatenate([lax.ppermute(tail, axis, [(i, (i + 1) % count) for i in...  2.87 us
  transfers between devices with their start and end apart: 8, of which 2 were waited for; matrix products, arithmetic and copies ran while one was open for 1% of the time, Pallas kernels for 0%

commit v1 on v0

--- a/solution.py
+++ b/solution.py
@@ -5,6 +5,11 @@
 
 DILATION_STEP = 8
 epsilon = 1e-05
+
+
+def by_each_axis(x, axis_one, axis_two):
+    inner = lax.psum(x, axis_one)
+    return lax.psum(inner, axis_two)
 
 
 def with_halo(cells, sides, width):
@@ -47,9 +52,10 @@
     cell_count = (
         tap_sum_total.shape[1] * tap_sum_total.shape[2] * lax.axis_size("gx") * lax.axis_size("gy")
     )
-    first_sum, second_sum = lax.psum(
+    first_sum, second_sum = by_each_axis(
         (jnp.sum(tap_sum_total, axis=(1, 2)), jnp.sum(tap_sum_total * tap_sum_total, axis=(1, 2))),
-        ("gx", "gy"),
+        "gy",
+        "gx",
     )
     average = first_sum / cell_count
     spread = second_sum / cell_count - average * average

time: 141 us -> 141 us (level)
  no operation moved by 1% of the time
where the time goes in v1:
time: 141 us; the launch traced here: 140 us
  blocking collectives  106 us (75%)
  starting transfers between devices  8.9 us (6%)
  matrix products  7.38 us (5%)
  other arithmetic  7.08 us (5%)
  local copies, waits for them, and re-layouts  6.52 us (5%)
  waiting for transfers between devices  3.66 us (3%)
    psum x2, blocking collectives, by_each_axis(): return lax.psum(inner, axis_two)  65.5 us
    all_gather x1, blocking collectives, body(): everyone = lax.all_gather(residue_feats, 'gx', axis=0, tiled=True)  23.8 us
    all_to_all x1, blocking collectives, body(): lax.all_to_all(whole_rows, 'gx', split_axis=2, concat_axis=1, tiled=True)  16.9 us
    dot_general x18, matrix products, dilated(): jnp.einsum('oc,crw->orw', weights[filter_tap_index], window, preferred_el...  6.34 us
    ppermute x4, starting transfers between devices, with_halo(): lax.ppermute(tail, axis, [(i, (i + 1) % count) for i in range(ends)])  4.94 us
    ppermute x4, starting transfers between devices, with_halo(): lax.ppermute(head, axis, [((i + 1) % count, i) for i in range(ends)])  3.96 us
    ppermute x4, waiting for transfers between devices, with_halo(): lax.ppermute(head, axis, [((i + 1) % count, i) for i in range(ends)])  3.65 us
    concatenate x4, other arithmetic, with_halo(): jnp.concatenate([lax.ppermute(tail, axis, [(i, (i + 1) % count) for i in...  2.87 us
  transfers between devices with their start and end apart: 8, of which 2 were waited for; matrix products, arithmetic and copies ran while one was open for 1% of the time, Pallas kernels for 0%

profile of v1, /device:TPU:0, one launch (start us, length us, event | category | flops | bytes accessed | tf_op | source)
XLA Modules:
  0.0 140.1 jit_solution(18333366935052121485)
XLA Ops:
  0.0 0.0 copy-start
  0.0 23.8 %all_gather.4 = bf16[256,256]{1,0:T(8,128)(2,1)S(1)} all-gather(bf16[16,256]{1,0:T(8,128)(2,1)} %param.8), channel_id=1, replica_groups=mesh['grp'=2,'gx'=16,'gy'=1] {'gx'}, dimensions={0}, use_global_device_ids=true | all-gather | bytes 139264 | tf_op jit(solution)/shard_map/all_gather | solution.py:73
  23.8 0.9 fusion.13
  24.7 0.2 fusion.12
  24.9 1.3 add_convert_fusion
  26.2 2.3 %collective-permute-start = (bf16[64,8,256]{2,0,1:T(8,128)(2,1)S(1)}, bf16[64,8,256]{2,0,1:T(8,128)(2,1)S(1)}, u32[]{:S(2)}, u32[]{:S(2)}) collective-permute-start(bf16[64,8,256]{2,0,1:T(8,128)(2,1)S(1)} %get-tuple-element.23), channel_id=1, source_target_pairs={{0,1},{1,2},{2,3},{3,4},{4,5},{5,6},{6,7},{7,8},{8,9},{9,10},{10,1... | collective-permute-start | bytes 786440 | tf_op jit(solution)/shard_map/ppermute | solution.py:23
  28.5 1.3 collective-permute-start.1
  29.8 0.0 copy-done.5
  29.8 0.3 fusion.62
  30.1 0.0 collective-permute-done
  30.1 1.8 %collective-permute-done.1 = bf16[64,8,256]{2,0,1:T(8,128)(2,1)S(1)} collective-permute-done((bf16[64,8,256]{2,0,1:T(8,128)(2,1)S(1)}, bf16[64,8,256]{2,0,1:T(8,128)(2,1)S(1)}, u32[]{:S(2)}, u32[]{:S(2)}) %collective-permute-start.1) | collective-permute-done | bytes 262176 | tf_op jit(solution)/shard_map/ppermute | solution.py:25
  31.9 0.1 pad_maximum_fusion.2
  32.1 0.3 fusion.93
  32.3 0.7 collective-permute-start.2
  33.0 0.7 collective-permute-start.3
  33.7 0.3 fusion.45
  34.0 0.3 fusion.36
  34.3 0.0 collective-permute-done.2
  34.3 0.0 collective-permute-done.3
  34.3 1.3 maximum_maximum_fusion
  35.6 0.4 fusion.43
  36.0 0.4 fusion.34
  36.4 0.3 fusion.41
  36.7 0.3 fusion.38
  36.9 0.4 fusion.11
  37.3 0.0 copy-start.4
  37.3 0.7 fusion.91
  38.0 0.0 copy-start.3
  38.0 33.9 %all-reduce.1 = (f32[64]{0:T(128)S(1)}, f32[64]{0:T(128)S(1)}) all-reduce(f32[64]{0:T(128)S(1)} %get-tuple-element.8, f32[64]{0:T(128)S(1)} %get-tuple-element.7), channel_id=1, replica_groups=mesh['grp'=2,'gx'=16,'gy'=1] {'gx'}, use_global_device_ids=true, to_apply=%region_3.0 | all-reduce | flops 128 | bytes 1024 | tf_op jit(solution)/shard_map/psum | solution.py:12
  72.0 0.0 copy-done.4
  72.0 0.6 fusion.15
  72.6 1.3 collective-permute-start.4
  73.9 1.3 collective-permute-start.5
  75.2 0.3 fusion.52
  75.5 0.0 collective-permute-done.4
  75.5 1.8 %collective-permute-done.5 = bf16[64,8,256]{2,0,1:T(8,128)(2,1)S(1)} collective-permute-done((bf16[64,8,256]{2,0,1:T(8,128)(2,1)S(1)}, bf16[64,8,256]{2,0,1:T(8,128)(2,1)S(1)}, u32[]{:S(2)}, u32[]{:S(2)}) %collective-permute-start.5) | collective-permute-done | bytes 262176 | tf_op jit(solution)/shard_map/ppermute | solution.py:25
  77.4 0.1 pad_maximum_fusion.3
  77.5 0.3 fusion.92
  77.8 0.7 collective-permute-start.6
  78.5 0.7 collective-permute-start.7
  79.2 0.3 fusion.31
  79.4 0.3 fusion.22
  79.7 0.0 collective-permute-done.6
  79.7 0.0 collective-permute-done.7
  79.7 1.3 maximum_maximum_fusion.1
  81.0 0.4 fusion.29
  81.4 0.4 fusion.20
  81.8 0.3 fusion.27
  82.1 0.3 fusion.24
  82.3 0.4 fusion.5
  82.7 0.0 copy-start.1
  82.8 0.7 fusion.90
  83.4 31.5 %all-reduce = (f32[64]{0:T(128)S(1)}, f32[64]{0:T(128)S(1)}) all-reduce(f32[64]{0:T(128)S(1)} %get-tuple-element.6, f32[64]{0:T(128)S(1)} %get-tuple-element.5), channel_id=1, replica_groups=mesh['grp'=2,'gx'=16,'gy'=1] {'gx'}, use_global_device_ids=true, to_apply=%region_7.8 | all-reduce | flops 128 | bytes 1024 | tf_op jit(solution)/shard_map/psum | solution.py:12
  115.0 0.7 fusion.17
  115.7 1.0 copy.18
  116.7 0.7 reshape.32
  117.4 16.9 %all_to_all.4 = bf16[16,2,8192]{2,1,0:T(2,128)(2,1)S(1)} all-to-all(bf16[16,2,8192]{2,1,0:T(2,128)(2,1)S(1)} %reshape.32), channel_id=1, replica_groups=mesh['grp'=2,'gx'=16,'gy'=1] {'gx'}, dimensions={0} | all-to-all | bytes 1048576 | tf_op jit(solution)/shard_map/all_to_all | solution.py:90
  134.3 0.7 reshape.33
  135.0 0.3 copy.19
  135.2 0.2 convert_bitcast_fusion
  135.5 0.2 copy.20
  135.7 2.0 %copy.21 = f32[64,256,16]{1,0,2:T(8,128)} copy(f32[64,256,16]{0,2,1:T(8,128)S(1)} %bitcast.109) | data formatting | bytes 2097152 | tf_op jit(solution)/shard_map/convert_element_type | solution.py:93
  137.6 1.4 fusion.19
  139.0 1.1 copy.22
  (11 shorter events, 0.1 us)
Async XLA Ops:
  0.0 24.7 %copy-start = (bf16[256,64]{0,1:T(8,128)(2,1)S(1)}, bf16[256,64]{0,1:T(8,128)(2,1)}, u32[]{:S(2)}) copy-start(bf16[256,64]{0,1:T(8,128)(2,1)} %param.11) | copy-start | bytes 98308
  0.0 29.8 %copy-start.5 = (f32[2,64]{1,0:T(2,128)S(1)}, f32[2,64]{1,0:T(2,128)}, u32[]{:S(2)}) copy-start(f32[2,64]{1,0:T(2,128)} %param.15) | copy-start | bytes 1540
  0.0 29.8 %copy-start.2 = (bf16[9,64,64]{2,1,0:T(8,128)(2,1)S(1)}, bf16[9,64,64]{2,1,0:T(8,128)(2,1)}, u32[]{:S(2)}) copy-start(bf16[9,64,64]{2,1,0:T(8,128)(2,1)} %param.12) | copy-start | bytes 221188
  26.2 3.9 %collective-permute-start = (bf16[64,8,256]{2,0,1:T(8,128)(2,1)S(1)}, bf16[64,8,256]{2,0,1:T(8,128)(2,1)S(1)}, u32[]{:S(2)}, u32[]{:S(2)}) collective-permute-start(bf16[64,8,256]{2,0,1:T(8,128)(2,1)S(1)} %get-tuple-element.23), channel_id=1, source_target_pairs={{0,1},{1,2},{2,3},{3,4},{4,5},{5,6},{6,7},{7,8},{8,9},{9,10},{10,1... | collective-permute-start | bytes 786440 | tf_op jit(solution)/shard_map/ppermute | solution.py:23
  28.5 3.4 %collective-permute-start.1 = (bf16[64,8,256]{2,0,1:T(8,128)(2,1)S(1)}, bf16[64,8,256]{2,0,1:T(8,128)(2,1)S(1)}, u32[]{:S(2)}, u32[]{:S(2)}) collective-permute-start(bf16[64,8,256]{2,0,1:T(8,128)(2,1)S(1)} %get-tuple-element.24), channel_id=1, source_target_pairs={{1,0},{2,1},{3,2},{4,3},{5,4},{6,5},{7,6},{8,7},{9,8},{10,9},{11,1... | collective-permute-start | bytes 786440 | tf_op jit(solution)/shard_map/ppermute | solution.py:25
  32.3 1.9 %collective-permute-start.2 = (bf16[64,32,8]{2,0,1:T(8,128)(2,1)S(1)}, bf16[64,32,8]{2,0,1:T(8,128)(2,1)S(1)}, u32[]{:S(2)}, u32[]{:S(2)}) collective-permute-start(bf16[64,32,8]{2,0,1:T(8,128)(2,1)S(1)} %get-tuple-element.19), channel_id=1, source_target_pairs={} | collective-permute-start | bytes 98312 | tf_op jit(solution)/shard_map/ppermute | solution.py:23
  33.0 1.3 collective-permute-start.3
  37.3 34.6 %copy-start.4 = (f32[2,64]{1,0:T(2,128)S(1)}, f32[2,64]{1,0:T(2,128)}, u32[]{:S(2)}) copy-start(f32[2,64]{1,0:T(2,128)} %param.14) | copy-start | bytes 1540
  38.0 37.2 %copy-start.3 = (bf16[9,64,64]{2,1,0:T(8,128)(2,1)S(1)}, bf16[9,64,64]{2,1,0:T(8,128)(2,1)}, u32[]{:S(2)}) copy-start(bf16[9,64,64]{2,1,0:T(8,128)(2,1)} %param.13) | copy-start | bytes 221188
  72.6 2.9 %collective-permute-start.4 = (bf16[64,8,256]{2,0,1:T(8,128)(2,1)S(1)}, bf16[64,8,256]{2,0,1:T(8,128)(2,1)S(1)}, u32[]{:S(2)}, u32[]{:S(2)}) collective-permute-start(bf16[64,8,256]{2,0,1:T(8,128)(2,1)S(1)} %get-tuple-element.21), channel_id=1, source_target_pairs={{0,1},{1,2},{2,3},{3,4},{4,5},{5,6},{6,7},{7,8},{8,9},{9,10},{10,1... | collective-permute-start | bytes 786440 | tf_op jit(solution)/shard_map/ppermute | solution.py:23
  73.9 3.4 %collective-permute-start.5 = (bf16[64,8,256]{2,0,1:T(8,128)(2,1)S(1)}, bf16[64,8,256]{2,0,1:T(8,128)(2,1)S(1)}, u32[]{:S(2)}, u32[]{:S(2)}) collective-permute-start(bf16[64,8,256]{2,0,1:T(8,128)(2,1)S(1)} %get-tuple-element.22), channel_id=1, source_target_pairs={{1,0},{2,1},{3,2},{4,3},{5,4},{6,5},{7,6},{8,7},{9,8},{10,9},{11,1... | collective-permute-start | bytes 786440 | tf_op jit(solution)/shard_map/ppermute | solution.py:25
  77.8 1.9 %collective-permute-start.6 = (bf16[64,32,8]{2,0,1:T(8,128)(2,1)S(1)}, bf16[64,32,8]{2,0,1:T(8,128)(2,1)S(1)}, u32[]{:S(2)}, u32[]{:S(2)}) collective-permute-start(bf16[64,32,8]{2,0,1:T(8,128)(2,1)S(1)} %get-tuple-element.15), channel_id=1, source_target_pairs={} | collective-permute-start | bytes 98312 | tf_op jit(solution)/shard_map/ppermute | solution.py:23
  78.5 1.3 collective-permute-start.7
  82.7 32.2 %copy-start.1 = (bf16[64,16,256]{2,1,0:T(8,128)(2,1)S(1)}, bf16[64,16,256]{2,1,0:T(8,128)(2,1)}, u32[]{:S(2)}) copy-start(bf16[64,16,256]{2,1,0:T(8,128)(2,1)} %param.9) | copy-start | bytes 1572868
